TPU v7x, 256 devices: a whole 4x4x8 slice. The times are simulated.
256 devices in a mesh: wide: 32 (over x, y, core), narrow: 8 (over z).
Axes of the slice: x: 4, y: 4, z: 8, core: 2. Of those that a mesh axis runs over, the one named last changes fastest.
Arguments:
- row_vectors: bfloat16 [32768, 2048], P('wide'), may hold values from -0.59765625 to 1.3984375
- col_vectors: bfloat16 [4096, 2048], P('narrow', 'wide'), may hold values from -0.59765625 to 1.3984375
- primal_matrix: bfloat16 [2048, 2048], P('wide'), may hold values from -1 to 3, as said below
- dual_inverse: bfloat16 [2048, 2048], P('wide'), may hold values from -1 to 3, as said below
Outputs:
- factored: float32 [32768, 4096], P('wide', 'narrow')
Inputs may be any that keep to these rules, and one draw needn't show every extreme that they name: `primal_matrix`: symmetric positive definite. `dual_inverse`: symmetric positive definite.
All inputs are finite; a program needn't handle non-finite values.
Results may differ from a plain program's by a relative error of at most 0.0027.
Values may be sent and summed in bfloat16 or wider, within the bound.
A program may use at most 64 MiB of HBM per device.

v0:
```python
import jax
import jax.numpy as jnp
from jax import lax
from jax.sharding import PartitionSpec as P


def from_everyone(x, axis):
    devices = lax.axis_size(axis)
    return lax.all_to_all(jnp.broadcast_to(x[None], (devices, *x.shape)), axis, 0, 0, tiled=True)


def joined_along(tiles, dim):
    shape = list(tiles.shape[1:])
    shape[dim] *= tiles.shape[0]
    return jnp.moveaxis(tiles, 0, dim).reshape(shape)


def gather_directly(x, axis, dim):
    tiles = from_everyone(x, axis)
    return joined_along(tiles, dim)


def broadcast(x, axis, root):
    return lax.dynamic_index_in_dim(lax.all_gather(x, axis), root, 0, keepdims=False)


def in_one_piece(arrays, axis, dim, along):
    both = jnp.concatenate(arrays, axis=along)
    whole, at, finished = (lax.all_gather(both, axis, axis=dim, tiled=True), 0, [])
    for a in arrays:
        finished.append(lax.slice_in_dim(whole, at, at + a.shape[along], axis=along))
        at += a.shape[along]
    return tuple(finished)


def spread(value, axis, source):
    kept = jnp.where(lax.axis_index(axis) == source, value, 0).astype(value.dtype)
    return lax.psum(kept, axis)


def per_device(row_vectors, col_vectors, primal_matrix, dual_inverse):
    wide_count = lax.axis_size("wide")
    wide_index = lax.axis_index("wide")
    narrow_index = lax.axis_index("narrow")
    cone_order = primal_matrix.shape[1]
    panel_width = col_vectors.shape[0]
    panel_share = panel_width // wide_count
    gram_scale = 16.0 / (cone_order * cone_order)
    column_set = gather_directly(col_vectors, "wide", 1)
    local_panel = lax.dynamic_slice_in_dim(column_set, wide_index * panel_share, panel_share, 0)
    panel_set = broadcast(local_panel, "narrow", 0)
    prod_primal = jnp.dot(primal_matrix, column_set.T, preferred_element_type=jnp.float32).astype(
        jnp.bfloat16
    )
    prod_dual = jnp.dot(dual_inverse, column_set.T, preferred_element_type=jnp.float32).astype(
        jnp.bfloat16
    )
    pieces = in_one_piece((prod_primal, prod_dual), "wide", 0, 1)
    row_slice = row_vectors
    panel_slice = panel_set
    gram_primal = jnp.dot(row_slice, pieces[0], preferred_element_type=jnp.float32)
    gram_dual = jnp.dot(row_slice, pieces[1], preferred_element_type=jnp.float32)
    tile_primal = jnp.dot(panel_slice, pieces[0], preferred_element_type=jnp.float32)
    tile_dual = jnp.dot(panel_slice, pieces[1], preferred_element_type=jnp.float32)
    slab = gram_primal * gram_dual * gram_scale
    panel_tile = tile_primal * tile_dual * gram_scale
    gram = gather_directly(panel_tile, "wide", 0)
    panel_primal, panel_dual = (spread(prod_primal, "narrow", 0), spread(prod_dual, "narrow", 0))
    pieces = in_one_piece((panel_primal, panel_dual), "wide", 0, 1)
    row_slice = row_vectors
    panel_slice = panel_set
    first_primal = jnp.dot(row_slice, pieces[0], preferred_element_type=jnp.float32)
    first_dual = jnp.dot(row_slice, pieces[1], preferred_element_type=jnp.float32)
    diag_primal = jnp.dot(panel_slice, pieces[0], preferred_element_type=jnp.float32)
    diag_dual = jnp.dot(panel_slice, pieces[1], preferred_element_type=jnp.float32)
    slab_first = first_primal * first_dual * gram_scale
    diag_share = diag_primal * diag_dual * gram_scale
    diag_block = gather_directly(diag_share, "wide", 0)
    factor = jnp.linalg.cholesky(diag_block)
    panel_cols = jax.scipy.linalg.solve_triangular(factor, slab_first.T, lower=True).T
    solved = jax.scipy.linalg.solve_triangular(factor, gram, lower=True)
    trailing = slab - jnp.dot(panel_cols, solved, precision=lax.Precision.HIGHEST)
    return jnp.where(narrow_index == 0, panel_cols, trailing)


def solution(mesh):
    placed = (P("wide", None), P("narrow", "wide"), P("wide", None), P("wide", None))
    return jax.shard_map(
        per_device, mesh=mesh, in_specs=placed, out_specs=P("wide", "narrow"), check_vma=False
    )
```

profile of v0, /device:TPU:1, one launch (start us, length us, event | category | flops | bytes accessed | tf_op | source)
XLA Modules:
  0.0 366.3 jit_solution(9703437709959540505)
XLA Ops:
  7.4 2.4 broadcast_in_dim.12
  9.8 8.6 %all-to-all-start = ((bf16[32,512,64]{1,2,0:T(8,128)(2,1)}), bf16[32,512,64]{1,2,0:T(8,128)(2,1)S(1)}, u32[]{:S(2)}, u32[]{:S(2)}) async-start(bf16[32,512,64]{1,2,0:T(8,128)(2,1)} %broadcast_in_dim.12), calls=%async_computation | async-start | bytes 4194304 | tf_op jit(solution)/shard_map/all_to_all | solution.py:9
  18.5 28.3 %all-to-all-done = bf16[32,512,64]{1,2,0:T(8,128)(2,1)S(1)} async-done(((bf16[32,512,64]{1,2,0:T(8,128)(2,1)}), bf16[32,512,64]{1,2,0:T(8,128)(2,1)S(1)}, u32[]{:S(2)}, u32[]{:S(2)}) %all-to-all-start) | async-done | bytes 2097184 | tf_op jit(solution)/shard_map/all_to_all | solution.py:9
  49.8 66.8 %all-reduce.4.cloned.1.call-done = (bf16[64,512]{1,0:T(8,128)(2,1)}, bf16[64,512]{1,0:T(8,128)(2,1)}) async-done(((bf16[64,512]{1,0:T(8,128)(2,1)}, bf16[64,512]{1,0:T(8,128)(2,1)}), (bf16[64,512]{1,0:T(8,128)(2,1)}, bf16[64,512]{1,0:T(8,128)(2,1)})) %all-reduce.4.cloned.1.call-update) | async-done | bytes 131088 | tf_op jit(solution)/shard_map/psum | solution.py:38
  118.5 19.7 %all-gather = bf16[128,2048]{1,0:T(8,128)(2,1)S(1)} all-gather(bf16[16,2048]{1,0:T(8,128)(2,1)S(1)} %copy.13), channel_id=2, replica_groups=mesh['wide'=32,'narrow'=8] {'narrow'}, dimensions={0}, use_global_device_ids=true | all-gather | bytes 589824 | tf_op jit(solution)/shard_map/all_gather | solution.py:24
  143.3 17.3 %all-to-all-start.2 = ((f32[32,16,512]{2,1,0:T(8,128)}), f32[32,16,512]{2,1,0:T(8,128)S(1)}, u32[]{:S(2)}, u32[]{:S(2)}) async-start(f32[32,16,512]{2,1,0:T(8,128)} %broadcast_in_dim.28), calls=%async_computation.2 | async-start | bytes 2097152 | tf_op jit(solution)/shard_map/all_to_all | solution.py:9
  160.7 7.0 %fusion.3 = f32[512,1024]{1,0:T(8,128)} fusion(bf16[1024,2048]{1,0:T(8,128)(2,1)} %param.4, bf16[2048,1024]{1,0:T(8,128)(2,1)} %all-gather.6.cloned.1.call-done), kind=kOutput, calls=%fused_computation.8 | convolution fusion | flops 2147483648 | bytes 8388608 | tf_op jit(solution)/shard_map/dot_general | solution.py:62
  167.6 3.7 %fusion.7 = f32[512,1024]{1,0:T(8,128)} fusion(bf16[1024,2048]{1,0:T(8,128)(2,1)S(1)} %copy-done.9, bf16[2048,1024]{1,0:T(8,128)(2,1)S(1)} %copy-done.2), kind=kOutput, calls=%fused_computation.12 | convolution fusion | flops 2147483648 | bytes 8388608 | tf_op jit(solution)/shard_map/dot_general | solution.py:61
  171.3 9.7 %all-gather.4.cloned.1.call-done = bf16[2048,1024]{1,0:T(8,128)(2,1)} async-done(((bf16[64,1024]{1,0:T(8,128)(2,1)}), bf16[2048,1024]{1,0:T(8,128)(2,1)}) %all-gather.4.cloned.1.call-update) | async-done | bytes 4194320 | tf_op jit(solution)/shard_map/all_gather | solution.py:29
  186.1 6.1 %all-to-all-start.1 = ((f32[32,16,512]{2,1,0:T(8,128)}), f32[32,16,512]{2,1,0:T(8,128)S(1)}, u32[]{:S(2)}, u32[]{:S(2)}) async-start(f32[32,16,512]{2,1,0:T(8,128)} %broadcast_in_dim.14), calls=%async_computation.1 | async-start | bytes 2097152 | tf_op jit(solution)/shard_map/all_to_all | solution.py:9
  192.2 5.3 %fusion.9 = f32[512,1024]{1,0:T(8,128)S(1)} fusion(bf16[1024,2048]{1,0:T(8,128)(2,1)} %param.4, bf16[2048,1024]{1,0:T(8,128)(2,1)} %all-gather.4.cloned.1.call-done), kind=kOutput, calls=%fused_computation.14 | convolution fusion | flops 2147483648 | bytes 8388608 | tf_op jit(solution)/shard_map/dot_general | solution.py:73
  197.6 3.8 %multiply_multiply_fusion = f32[512,1024]{1,0:T(8,128)} fusion(f32[512,1024]{1,0:T(8,128)S(1)} %fusion.9, bf16[1024,2048]{1,0:T(8,128)(2,1)S(1)} %copy-done.10, bf16[2048,1024]{1,0:T(8,128)(2,1)S(1)} %copy-done.1), kind=kOutput, calls=%fused_computation.5 | convolution fusion | flops 2148532224 | bytes 10485760 | tf_op jit(solution)/shard_map/dot_general | solution.py:72
  202.4 6.6 %all-to-all-done.1 = f32[32,16,512]{2,1,0:T(8,128)S(1)} async-done(((f32[32,16,512]{2,1,0:T(8,128)}), f32[32,16,512]{2,1,0:T(8,128)S(1)}, u32[]{:S(2)}, u32[]{:S(2)}) %all-to-all-start.1) | async-done | bytes 1048608 | tf_op jit(solution)/shard_map/all_to_all | solution.py:9
  209.6 11.7 %cholesky.104 = f32[128,128]{1,0:T(8,128)S(1)} custom-call(f32[128,128]{1,0:T(8,128)S(1)} %cholesky.266), custom_call_target="Cholesky" | custom-call | tf_op jit(solution)/shard_map/jit(cholesky)/cholesky | solution.py:79
  221.4 9.8 %custom-call.34 = f32[1,128,128]{1,2,0:T(8,128)S(1)} custom-call(f32[1,128,128]{2,1,0:T(8,128)S(1)} %get-tuple-element.38), custom_call_target="InvertDiagBlocksLowerTriangular" | custom-call | tf_op jit(solution)/shard_map/jit(cholesky)/cholesky | solution.py:79
  232.1 11.7 %cholesky.217 = f32[128,128]{1,0:T(8,128)S(1)} custom-call(f32[128,128]{1,0:T(8,128)S(1)} %cholesky.270), custom_call_target="Cholesky" | custom-call | tf_op jit(solution)/shard_map/jit(cholesky)/cholesky | solution.py:79
  243.9 9.8 %custom-call.35 = f32[1,128,128]{1,2,0:T(8,128)S(1)} custom-call(f32[1,128,128]{2,1,0:T(8,128)S(1)} %get-tuple-element.35), custom_call_target="InvertDiagBlocksLowerTriangular" | custom-call | tf_op jit(solution)/shard_map/jit(cholesky)/cholesky | solution.py:79
  254.4 11.7 %cholesky.238 = f32[128,128]{1,0:T(8,128)S(1)} custom-call(f32[128,128]{1,0:T(8,128)S(1)} %cholesky.275), custom_call_target="Cholesky" | custom-call | tf_op jit(solution)/shard_map/jit(cholesky)/cholesky | solution.py:79
  266.8 10.2 %custom-call.36 = f32[1,128,128]{1,2,0:T(8,128)S(1)} custom-call(f32[1,128,128]{2,1,0:T(8,128)S(1)} %get-tuple-element.32), custom_call_target="InvertDiagBlocksLowerTriangular" | custom-call | tf_op jit(solution)/shard_map/jit(cholesky)/cholesky | solution.py:79
  277.6 11.7 %cholesky.255 = f32[128,128]{1,0:T(8,128)S(1)} custom-call(f32[128,128]{1,0:T(8,128)S(1)} %convolution_subtract_fusion.7), custom_call_target="Cholesky" | custom-call | tf_op jit(solution)/shard_map/jit(cholesky)/cholesky | solution.py:79
  293.6 10.7 %while.1 = (s32[]{:T(128)}, f32[512,512]{1,0:T(8,128)S(1)}, s32[4,2]{0,1:T(2,128)S(1)}, f32[4,128,128]{2,1,0:T(8,128)}, s32[]{:T(128)}) while((s32[]{:T(128)}, f32[512,512]{1,0:T(8,128)S(1)}, s32[4,2]{0,1:T(2,128)S(1)}, f32[4,128,128]{2,1,0:T(8,128)}, s32[]{:T(128)}) %tuple.32), condition=%wide.while_cond, body=%wide.while_body.sunk | while | flops 2 | bytes 132705 | solution.py:80
  299.6 2.0 bitcast_dynamic-update-slice_fusion.2
  304.3 40.3 %custom-call.37 = f32[4,128,128]{1,2,0:T(8,128)S(1)} custom-call(f32[4,128,128]{2,1,0:T(8,128)} %get-tuple-element.12), custom_call_target="InvertDiagBlocksLowerTriangular" | custom-call | tf_op jit(solution)/shard_map/jit(_solve_triangular)/triangular_solve | solution.py:80
  352.9 4.0 %fusion = f32[1024,512]{0,1:T(8,128)S(1)} fusion(f32[512,1024]{1,0:T(8,128)S(1)} %copy-done.12, f32[512,1024]{1,0:T(8,128)S(1)} %copy-done.11, f32[128,1024]{1,0:T(8,128)S(1)} %fusion.82, f32[128,1024]{1,0:T(8,128)S(1)} %fusion.80, f32[128,1024]{1,0:T(8,128)S(1)} %fusion.78, f32[128,1024]{1,0:T(8,128)S(1)} %fusion.56, f32[128,512]{1,0:T(8,128)S(1)} %fusion.81, ...), kind=kOutput, calls=%fused_computation.4 | convolution fusion | flops 3227254784 | bytes 9437185 | tf_op jit(solution)/shard_map/dot_general | solution.py:82
  (96 shorter events, 39.9 us)
Async XLA Ops:
  7.4 39.4 %copy-start = (bf16[64,2048]{1,0:T(8,128)(2,1)S(1)}, bf16[64,2048]{1,0:T(8,128)(2,1)}, u32[]{:S(2)}) copy-start(bf16[64,2048]{1,0:T(8,128)(2,1)} %param.7) | copy-start | bytes 786436
  9.8 36.9 %all-to-all-start = ((bf16[32,512,64]{1,2,0:T(8,128)(2,1)}), bf16[32,512,64]{1,2,0:T(8,128)(2,1)S(1)}, u32[]{:S(2)}, u32[]{:S(2)}) async-start(bf16[32,512,64]{1,2,0:T(8,128)(2,1)} %broadcast_in_dim.12), calls=%async_computation | async-start | bytes 4194304 | tf_op jit(solution)/shard_map/all_to_all | solution.py:9
  18.4 29.5 %copy-start.8 = (bf16[64,2048]{1,0:T(8,128)(2,1)S(1)}, bf16[64,2048]{1,0:T(8,128)(2,1)}, u32[]{:S(2)}) copy-start(bf16[64,2048]{1,0:T(8,128)(2,1)} %param.6) | copy-start | bytes 786436
  18.4 98.2 %all-reduce.4.cloned.1.call-start = ((), (), s32[]{:S(2)}) async-start(), calls=%async_computation.5 | async-start | bytes 262144 | tf_op jit(solution)/shard_map/psum | solution.py:38
  49.0 89.3 %all-gather.6.cloned.1.call-start = ((), (), s32[]{:S(2)}) async-start(), calls=%async_computation.4 | async-start | bytes 4325376 | tf_op jit(solution)/shard_map/all_gather | solution.py:29
  49.7 131.3 %all-gather.4.cloned.1.call-start = ((), (), s32[]{:S(2)}) async-start(), calls=%async_computation.3 | async-start | bytes 4325376 | tf_op jit(solution)/shard_map/all_gather | solution.py:29
  143.3 41.7 %all-to-all-start.2 = ((f32[32,16,512]{2,1,0:T(8,128)}), f32[32,16,512]{2,1,0:T(8,128)S(1)}, u32[]{:S(2)}, u32[]{:S(2)}) async-start(f32[32,16,512]{2,1,0:T(8,128)} %broadcast_in_dim.28), calls=%async_computation.2 | async-start | bytes 2097152 | tf_op jit(solution)/shard_map/all_to_all | solution.py:9
  160.7 7.0 %copy-start.2 = (bf16[2048,1024]{1,0:T(8,128)(2,1)S(1)}, bf16[2048,1024]{1,0:T(8,128)(2,1)}, u32[]{:S(2)}) copy-start(bf16[2048,1024]{1,0:T(8,128)(2,1)} %all-gather.6.cloned.1.call-done) | copy-start | bytes 12582916
  160.7 7.0 %copy-start.9 = (bf16[1024,2048]{1,0:T(8,128)(2,1)S(1)}, bf16[1024,2048]{1,0:T(8,128)(2,1)}, u32[]{:S(2)}) copy-start(bf16[1024,2048]{1,0:T(8,128)(2,1)} %param.4) | copy-start | bytes 12582916
  186.1 22.9 %all-to-all-start.1 = ((f32[32,16,512]{2,1,0:T(8,128)}), f32[32,16,512]{2,1,0:T(8,128)S(1)}, u32[]{:S(2)}, u32[]{:S(2)}) async-start(f32[32,16,512]{2,1,0:T(8,128)} %broadcast_in_dim.14), calls=%async_computation.1 | async-start | bytes 2097152 | tf_op jit(solution)/shard_map/all_to_all | solution.py:9
  192.2 5.4 %copy-start.1 = (bf16[2048,1024]{1,0:T(8,128)(2,1)S(1)}, bf16[2048,1024]{1,0:T(8,128)(2,1)}, u32[]{:S(2)}) copy-start(bf16[2048,1024]{1,0:T(8,128)(2,1)} %all-gather.4.cloned.1.call-done) | copy-start | bytes 12582916
  192.2 5.4 %copy-start.10 = (bf16[1024,2048]{1,0:T(8,128)(2,1)S(1)}, bf16[1024,2048]{1,0:T(8,128)(2,1)}, u32[]{:S(2)}) copy-start(bf16[1024,2048]{1,0:T(8,128)(2,1)} %param.4) | copy-start | bytes 12582916
  254.3 90.3 %copy-start.5 = (f32[8,16,512]{2,1,0:T(8,128)S(1)}, f32[8,16,512]{2,1,0:T(8,128)}, u32[]{:S(2)}) copy-start(f32[8,16,512]{2,1,0:T(8,128)} %get-tuple-element.25) | copy-start | bytes 786436
  277.0 68.1 %copy-start.4 = (f32[8,16,512]{2,1,0:T(8,128)S(1)}, f32[8,16,512]{2,1,0:T(8,128)}, u32[]{:S(2)}) copy-start(f32[8,16,512]{2,1,0:T(8,128)} %get-tuple-element.28) | copy-start | bytes 786436
  293.4 52.5 %copy-start.7 = (f32[8,16,512]{2,1,0:T(8,128)S(1)}, f32[8,16,512]{2,1,0:T(8,128)}, u32[]{:S(2)}) copy-start(f32[8,16,512]{2,1,0:T(8,128)} %get-tuple-element.27) | copy-start | bytes 786436
  304.3 42.5 %copy-start.6 = (f32[8,16,512]{2,1,0:T(8,128)S(1)}, f32[8,16,512]{2,1,0:T(8,128)}, u32[]{:S(2)}) copy-start(f32[8,16,512]{2,1,0:T(8,128)} %get-tuple-element.26) | copy-start | bytes 786436
  345.5 2.4 copy-start.3
  350.5 2.4 copy-start.12
  351.1 1.8 copy-start.11
Sparse Core Ops, SparseCore 0:
  49.1 67.4 all-reduce.3
Sparse Core Ops, SparseCore 1:
  52.0 50.4 all-gather.5
  118.2 62.8 all-gather.3
where the time goes:
time: 373 us; the launch traced here: 366 us
  other arithmetic  122 us (33%)
  waiting for transfers between devices  111 us (30%)
  matrix products  43.9 us (12%)
  starting transfers between devices  32.2 us (9%)
  blocking collectives  19.7 us (5%)
  local copies, waits for them, and re-layouts  19.1 us (5%)
  between operations  18.1 us (5%)
    another operation x14, other arithmetic, per_device(): factor = jnp.linalg.cholesky(diag_block)  78.9 us
    psum x1, waiting for transfers between devices, spread(): return lax.psum(kept, axis)  66.8 us
    another operation x3, other arithmetic, per_device(): jax.scipy.linalg.solve_triangular(factor, slab_first.T, lower=True)  40.5 us
    all_to_all x3, waiting for transfers between devices, from_everyone(): lax.all_to_all(jnp.broadcast_to(x[None], (devices, *x.shape)), axis, 0, 0...  34.9 us
    all_to_all x3, starting transfers between devices, from_everyone(): lax.all_to_all(jnp.broadcast_to(x[None], (devices, *x.shape)), axis, 0, 0...  32 us
    all_gather x1, blocking collectives, broadcast(): lax.all_gather(x, axis)  19.7 us
    dot_general x2, matrix products, per_device(): jnp.dot(row_slice, pieces[1], preferred_element_type=jnp.float32)  12.3 us
    another operation x12, local copies, waits for them, and re-layouts  10.7 us
  transfers between devices with their start and end apart: 6, of which 4 were waited for; matrix products, arithmetic and copies ran while one was open for 9% of the time, Pallas kernels for 0%

commit v1 on v0

--- a/solution.py
+++ b/solution.py
@@ -35,7 +35,7 @@
 
 def spread(value, axis, source):
     kept = jnp.where(lax.axis_index(axis) == source, value, 0).astype(value.dtype)
-    return lax.psum(kept, axis)
+    return jnp.sum(lax.all_gather(kept, axis), axis=0)
 
 
 def per_device(row_vectors, col_vectors, primal_matrix, dual_inverse):

time: 373 us -> 394 us (1.056)
  blocking collectives: 19.7 us -> 61.4 us
  starting transfers between devices: 32.2 us -> 19.8 us
  waiting for transfers between devices: 111 us -> 106 us
    all_gather x2, waiting for transfers between devices: 9.7 us -> 78.1 us  [in_one_piece(): lax.all_gather(both, axis, axis=dim, tiled=True)]
    psum x1 -> x0, waiting for transfers between devices: 66.8 us -> none  [spread(): return lax.psum(kept, axis)]
    all_gather x0 -> x2, blocking collectives: none -> 42 us  [spread(): return jnp.sum(lax.all_gather(kept, axis), axis=0)]
    all_to_all x3, starting transfers between devices: 32 us -> 19.7 us  [from_everyone(): lax.all_to_all(jnp.broadcast_to(x[None], (devices, *x.shape)), axis, 0, 0...]
    all_to_all x3, waiting for transfers between devices: 34.9 us -> 28.3 us  [from_everyone(): lax.all_to_all(jnp.broadcast_to(x[None], (devices, *x.shape)), axis, 0, 0...]
  transfers between devices with their start and end apart: 6 -> 5, of which waited for: 4 -> 3; matrix products, arithmetic and copies ran while one was open for 9% -> 42% of each run, Pallas kernels for 0% -> 0%
where the time goes in v1:
time: 394 us; the launch traced here: 390 us
  other arithmetic  122 us (31%)
  waiting for transfers between devices  106 us (27%)
  blocking collectives  61.4 us (16%)
  matrix products  43.8 us (11%)
  local copies, waits for them, and re-layouts  20 us (5%)
  starting transfers between devices  19.8 us (5%)
  between operations  16.6 us (4%)
    another operation x14, other arithmetic, per_device(): factor = jnp.linalg.cholesky(diag_block)  78.8 us
    all_gather x2, waiting for transfers between devices, in_one_piece(): lax.all_gather(both, axis, axis=dim, tiled=True)  78.1 us
    all_gather x2, blocking collectives, spread(): return jnp.sum(lax.all_gather(kept, axis), axis=0)  42 us
    another operation x3, other arithmetic, per_device(): jax.scipy.linalg.solve_triangular(factor, slab_first.T, lower=True)  40.3 us
    all_to_all x3, waiting for transfers between devices, from_everyone(): lax.all_to_all(jnp.broadcast_to(x[None], (devices, *x.shape)), axis, 0, 0...  28.3 us
    all_to_all x3, starting transfers between devices, from_everyone(): lax.all_to_all(jnp.broadcast_to(x[None], (devices, *x.shape)), axis, 0, 0...  19.7 us
    all_gather x1, blocking collectives, broadcast(): lax.all_gather(x, axis)  19.4 us
    dot_general x2, matrix products, per_device(): jnp.dot(row_slice, pieces[1], preferred_element_type=jnp.float32)  13.2 us
  transfers between devices with their start and end apart: 5, of which 3 were waited for; matrix products, arithmetic and copies ran while one was open for 42% of the time, Pallas kernels for 0%

profile of v1, /device:TPU:1, one launch (start us, length us, event | category | flops | bytes accessed | tf_op | source)
XLA Modules:
  0.0 390.1 jit_solution(17799929784607261935)
XLA Ops:
  6.5 2.4 broadcast_in_dim.12
  9.0 8.6 %all-to-all-start = ((bf16[32,512,64]{1,2,0:T(8,128)(2,1)}), bf16[32,512,64]{1,2,0:T(8,128)(2,1)S(1)}, u32[]{:S(2)}, u32[]{:S(2)}) async-start(bf16[32,512,64]{1,2,0:T(8,128)(2,1)} %broadcast_in_dim.12), calls=%async_computation | async-start | bytes 4194304 | tf_op jit(solution)/shard_map/all_to_all | solution.py:9
  17.6 28.3 %all-to-all-done = bf16[32,512,64]{1,2,0:T(8,128)(2,1)S(1)} async-done(((bf16[32,512,64]{1,2,0:T(8,128)(2,1)}), bf16[32,512,64]{1,2,0:T(8,128)(2,1)S(1)}, u32[]{:S(2)}, u32[]{:S(2)}) %all-to-all-start) | async-done | bytes 2097184 | tf_op jit(solution)/shard_map/all_to_all | solution.py:9
  46.4 23.1 %all-gather.1 = bf16[512,512]{1,0:T(8,128)(2,1)S(1)} all-gather(bf16[64,512]{1,0:T(8,128)(2,1)S(1)} %get-tuple-element.39), channel_id=3, replica_groups=mesh['wide'=32,'narrow'=8] {'narrow'}, dimensions={0}, use_global_device_ids=true | all-gather | bytes 589824 | tf_op jit(solution)/shard_map/all_gather | solution.py:38
  70.0 18.9 %all-gather.2 = bf16[512,512]{1,0:T(8,128)(2,1)S(1)} all-gather(bf16[64,512]{1,0:T(8,128)(2,1)S(1)} %get-tuple-element.37), channel_id=4, replica_groups=mesh['wide'=32,'narrow'=8] {'narrow'}, dimensions={0}, use_global_device_ids=true | all-gather | bytes 589824 | tf_op jit(solution)/shard_map/all_gather | solution.py:38
  92.4 19.4 %all-gather = bf16[128,2048]{1,0:T(8,128)(2,1)S(1)} all-gather(bf16[16,2048]{1,0:T(8,128)(2,1)S(1)} %copy.13), channel_id=2, replica_groups=mesh['wide'=32,'narrow'=8] {'narrow'}, dimensions={0}, use_global_device_ids=true | all-gather | bytes 589824 | tf_op jit(solution)/shard_map/all_gather | solution.py:24
  111.8 38.6 %all-gather.6.cloned.1.call-done = bf16[2048,1024]{1,0:T(8,128)(2,1)} async-done(((bf16[64,1024]{1,0:T(8,128)(2,1)}), bf16[2048,1024]{1,0:T(8,128)(2,1)}) %all-gather.6.cloned.1.call-update) | async-done | bytes 4194320 | tf_op jit(solution)/shard_map/all_gather | solution.py:29
  155.5 5.6 %all-to-all-start.1 = ((f32[32,16,512]{2,1,0:T(8,128)}), f32[32,16,512]{2,1,0:T(8,128)S(1)}, u32[]{:S(2)}, u32[]{:S(2)}) async-start(f32[32,16,512]{2,1,0:T(8,128)} %broadcast_in_dim.14), calls=%async_computation.1 | async-start | bytes 2097152 | tf_op jit(solution)/shard_map/all_to_all | solution.py:9
  161.1 6.5 %fusion.9 = f32[512,1024]{1,0:T(8,128)} fusion(bf16[1024,2048]{1,0:T(8,128)(2,1)} %param.4, bf16[2048,1024]{1,0:T(8,128)(2,1)} %all-gather.6.cloned.1.call-done), kind=kOutput, calls=%fused_computation.14 | convolution fusion | flops 2147483648 | bytes 8388608 | tf_op jit(solution)/shard_map/dot_general | solution.py:73
  167.6 39.5 %all-gather.8.cloned.1.call-done = bf16[2048,1024]{1,0:T(8,128)(2,1)} async-done(((bf16[64,1024]{1,0:T(8,128)(2,1)}), bf16[2048,1024]{1,0:T(8,128)(2,1)}) %all-gather.8.cloned.1.call-update) | async-done | bytes 4194320 | tf_op jit(solution)/shard_map/all_gather | solution.py:29
  207.1 6.7 %fusion.3 = f32[512,1024]{1,0:T(8,128)} fusion(bf16[1024,2048]{1,0:T(8,128)(2,1)} %param.4, bf16[2048,1024]{1,0:T(8,128)(2,1)} %all-gather.8.cloned.1.call-done), kind=kOutput, calls=%fused_computation.8 | convolution fusion | flops 2147483648 | bytes 8388608 | tf_op jit(solution)/shard_map/dot_general | solution.py:62
  213.8 3.7 fusion.7
  219.7 3.7 multiply_multiply_fusion
  224.5 5.5 %all-to-all-start.2 = ((f32[32,16,512]{2,1,0:T(8,128)}), f32[32,16,512]{2,1,0:T(8,128)S(1)}, u32[]{:S(2)}, u32[]{:S(2)}) async-start(f32[32,16,512]{2,1,0:T(8,128)} %broadcast_in_dim.28), calls=%async_computation.2 | async-start | bytes 2097152 | tf_op jit(solution)/shard_map/all_to_all | solution.py:9
  231.6 11.7 %cholesky.104 = f32[128,128]{1,0:T(8,128)S(1)} custom-call(f32[128,128]{1,0:T(8,128)S(1)} %cholesky.266), custom_call_target="Cholesky" | custom-call | tf_op jit(solution)/shard_map/jit(cholesky)/cholesky | solution.py:79
  243.5 9.8 %custom-call.34 = f32[1,128,128]{1,2,0:T(8,128)S(1)} custom-call(f32[1,128,128]{2,1,0:T(8,128)S(1)} %get-tuple-element.36), custom_call_target="InvertDiagBlocksLowerTriangular" | custom-call | tf_op jit(solution)/shard_map/jit(cholesky)/cholesky | solution.py:79
  255.8 11.7 %cholesky.217 = f32[128,128]{1,0:T(8,128)S(1)} custom-call(f32[128,128]{1,0:T(8,128)S(1)} %cholesky.270), custom_call_target="Cholesky" | custom-call | tf_op jit(solution)/shard_map/jit(cholesky)/cholesky | solution.py:79
  267.6 10.2 %custom-call.35 = f32[1,128,128]{1,2,0:T(8,128)S(1)} custom-call(f32[1,128,128]{2,1,0:T(8,128)S(1)} %get-tuple-element.33), custom_call_target="InvertDiagBlocksLowerTriangular" | custom-call | tf_op jit(solution)/shard_map/jit(cholesky)/cholesky | solution.py:79
  279.4 11.7 %cholesky.238 = f32[128,128]{1,0:T(8,128)S(1)} custom-call(f32[128,128]{1,0:T(8,128)S(1)} %cholesky.275), custom_call_target="Cholesky" | custom-call | tf_op jit(solution)/shard_map/jit(cholesky)/cholesky | solution.py:79
  291.8 9.8 %custom-call.36 = f32[1,128,128]{1,2,0:T(8,128)S(1)} custom-call(f32[1,128,128]{2,1,0:T(8,128)S(1)} %get-tuple-element.30), custom_call_target="InvertDiagBlocksLowerTriangular" | custom-call | tf_op jit(solution)/shard_map/jit(cholesky)/cholesky | solution.py:79
  303.1 11.7 %cholesky.255 = f32[128,128]{1,0:T(8,128)S(1)} custom-call(f32[128,128]{1,0:T(8,128)S(1)} %convolution_subtract_fusion.7), custom_call_target="Cholesky" | custom-call | tf_op jit(solution)/shard_map/jit(cholesky)/cholesky | solution.py:79
  318.8 10.1 %while.1 = (s32[]{:T(128)}, f32[512,512]{1,0:T(8,128)S(1)}, s32[4,2]{0,1:T(2,128)S(1)}, f32[4,128,128]{2,1,0:T(8,128)}, s32[]{:T(128)}) while((s32[]{:T(128)}, f32[512,512]{1,0:T(8,128)S(1)}, s32[4,2]{0,1:T(2,128)S(1)}, f32[4,128,128]{2,1,0:T(8,128)}, s32[]{:T(128)}) %tuple.32), condition=%wide.while_cond, body=%wide.while_body.sunk | while | flops 2 | bytes 132705 | solution.py:80
  328.9 40.1 %custom-call.37 = f32[4,128,128]{1,2,0:T(8,128)S(1)} custom-call(f32[4,128,128]{2,1,0:T(8,128)} %get-tuple-element.12), custom_call_target="InvertDiagBlocksLowerTriangular" | custom-call | tf_op jit(solution)/shard_map/jit(_solve_triangular)/triangular_solve | solution.py:80
  377.3 4.0 %fusion = f32[1024,512]{0,1:T(8,128)S(1)} fusion(f32[512,1024]{1,0:T(8,128)S(1)} %copy-done.8, f32[512,1024]{1,0:T(8,128)S(1)} %copy-done.7, f32[128,1024]{1,0:T(8,128)S(1)} %fusion.82, f32[128,1024]{1,0:T(8,128)S(1)} %fusion.80, f32[128,1024]{1,0:T(8,128)S(1)} %fusion.78, f32[128,1024]{1,0:T(8,128)S(1)} %fusion.56, f32[128,512]{1,0:T(8,128)S(1)} %fusion.81, ...), kind=kOutput, calls=%fused_computation.4 | convolution fusion | flops 3227254784 | bytes 9437185 | tf_op jit(solution)/shard_map/dot_general | solution.py:82
  (91 shorter events, 42.3 us)
Async XLA Ops:
  6.5 39.4 %copy-start = (bf16[64,2048]{1,0:T(8,128)(2,1)S(1)}, bf16[64,2048]{1,0:T(8,128)(2,1)}, u32[]{:S(2)}) copy-start(bf16[64,2048]{1,0:T(8,128)(2,1)} %param.6) | copy-start | bytes 786436
  9.0 36.9 %all-to-all-start = ((bf16[32,512,64]{1,2,0:T(8,128)(2,1)}), bf16[32,512,64]{1,2,0:T(8,128)(2,1)S(1)}, u32[]{:S(2)}, u32[]{:S(2)}) async-start(bf16[32,512,64]{1,2,0:T(8,128)(2,1)} %broadcast_in_dim.12), calls=%async_computation | async-start | bytes 4194304 | tf_op jit(solution)/shard_map/all_to_all | solution.py:9
  17.6 52.0 %copy-start.5 = (bf16[64,2048]{1,0:T(8,128)(2,1)S(1)}, bf16[64,2048]{1,0:T(8,128)(2,1)}, u32[]{:S(2)}) copy-start(bf16[64,2048]{1,0:T(8,128)(2,1)} %param.7) | copy-start | bytes 786436
  17.6 132.8 %all-gather.6.cloned.1.call-start = ((), (), s32[]{:S(2)}) async-start(), calls=%async_computation.3 | async-start | bytes 4325376 | tf_op jit(solution)/shard_map/all_gather | solution.py:29
  91.2 115.9 %all-gather.8.cloned.1.call-start = ((), (), s32[]{:S(2)}) async-start(), calls=%async_computation.4 | async-start | bytes 4325376 | tf_op jit(solution)/shard_map/all_gather | solution.py:29
  155.5 67.9 %all-to-all-start.1 = ((f32[32,16,512]{2,1,0:T(8,128)}), f32[32,16,512]{2,1,0:T(8,128)S(1)}, u32[]{:S(2)}, u32[]{:S(2)}) async-start(f32[32,16,512]{2,1,0:T(8,128)} %broadcast_in_dim.14), calls=%async_computation.1 | async-start | bytes 2097152 | tf_op jit(solution)/shard_map/all_to_all | solution.py:9
  207.1 6.7 %copy-start.2 = (bf16[2048,1024]{1,0:T(8,128)(2,1)S(1)}, bf16[2048,1024]{1,0:T(8,128)(2,1)}, u32[]{:S(2)}) copy-start(bf16[2048,1024]{1,0:T(8,128)(2,1)} %all-gather.8.cloned.1.call-done) | copy-start | bytes 12582916
  207.1 6.7 %copy-start.6 = (bf16[1024,2048]{1,0:T(8,128)(2,1)S(1)}, bf16[1024,2048]{1,0:T(8,128)(2,1)}, u32[]{:S(2)}) copy-start(bf16[1024,2048]{1,0:T(8,128)(2,1)} %param.4) | copy-start | bytes 12582916
  213.8 4.5 %copy-start.9 = (f32[512,1024]{1,0:T(8,128)S(1)}, f32[512,1024]{1,0:T(8,128)}, u32[]{:S(2)}) copy-start(f32[512,1024]{1,0:T(8,128)} %fusion.9) | copy-start | bytes 6291460
  217.5 2.2 copy-start.1
  224.5 144.5 %all-to-all-start.2 = ((f32[32,16,512]{2,1,0:T(8,128)}), f32[32,16,512]{2,1,0:T(8,128)S(1)}, u32[]{:S(2)}, u32[]{:S(2)}) async-start(f32[32,16,512]{2,1,0:T(8,128)} %broadcast_in_dim.28), calls=%async_computation.2 | async-start | bytes 2097152 | tf_op jit(solution)/shard_map/all_to_all | solution.py:9
  230.6 1.0 copy-start.3
  369.9 2.4 copy-start.4
  374.9 2.4 copy-start.8
  375.5 1.8 copy-start.7
Sparse Core Ops, SparseCore 0:
  91.3 59.0 all-gather.5
  152.9 54.0 all-gather.7
